TPU v7x, 32 devices: a whole 2x2x4 slice. The times are simulated.
32 devices in a mesh: slab: 8 (over z, core), sub: 4 (over y, x).
Axes of the slice: x: 2, y: 2, z: 4, core: 2. Of those that a mesh axis runs over, the one named last changes fastest.
Arguments:
- child_moments: bfloat16 [216, 32768], P(None, ('slab', 'sub')), may hold values from -6 to 6
- incoming: bfloat16 [216, 4096], P(None, ('slab', 'sub')), may hold values from -6 to 6
- m2m_ops: bfloat16 [8, 216, 216], replicated, may hold values from -0.15625 to 0.15625
- m2l_ops: bfloat16 [160, 216, 216], P('sub'), may hold values from -0.046875 to 0.046875
- l2l_ops: bfloat16 [8, 216, 216], replicated, may hold values from -0.4375 to 0.4375
- partners: int32 [160, 4096], P(None, ('slab', 'sub')), may hold values from -1 to 4095, as said below
Outputs:
- child_locals: float32 [216, 32768], P(None, ('slab', 'sub'))
Inputs may be any that keep to these rules, and one draw needn't show every extreme that they name: `partners`: cells are numbered in Morton order of bricks of the domain, each brick one cell wide along the first dimension; the source of a pair lies in the same slab as its target or in an adjacent one, that is its id divided by 128 * 4 differs from the target's by at most one. Pairs are those of the interaction list: source and target are not adjacent, their parents are.
All inputs are finite; a program needn't handle non-finite values.
Results may differ from a plain program's by a relative error of at most 0.0035.
Values may be sent and summed in bfloat16 or wider, within the bound.
No kernel may reach another device: no remote copies, remote signals or barrier semaphores. Data moves between devices by JAX's collectives and lax.ppermute only.
A program may use at most 128 MiB of HBM per device.

v0:
```python
import jax
import jax.numpy as jnp
from jax import lax
from jax.sharding import PartitionSpec as P


def extended_2(block, sides, width):
    for axis, dim in sides:
        count = lax.axis_size(axis)
        forward = [(i, i + 1) for i in range(count - 1)]
        backward = [(target, source) for source, target in forward]
        low = lax.ppermute(
            lax.slice_in_dim(block, block.shape[dim] - width, None, axis=dim), axis, forward
        )
        high = lax.ppermute(lax.slice_in_dim(block, 0, width, axis=dim), axis, backward)
        block = jnp.concatenate([low, block, high], axis=dim)
    return block


def local(child_moments, incoming, m2m_ops, m2l_ops, l2l_ops, partners):
    order_cube = child_moments.shape[0]
    cell_count = child_moments.shape[1] // 8
    children = child_moments.reshape(order_cube, cell_count, 8)
    moments = jnp.einsum(
        "oij,jpo->ip", m2m_ops, children, preferred_element_type=jnp.float32
    ).astype(jnp.bfloat16)
    sub_count = lax.axis_size("sub")
    my_slab = lax.axis_index("slab")
    rim_cols = 32
    facing = jnp.concatenate([moments[:, :rim_cols], moments[:, cell_count - rim_cols :]], axis=1)
    padded = extended_2(facing, (("slab", 1),), rim_cols)
    below_top = padded[:, :rim_cols]
    above_bottom = padded[:, padded.shape[1] - rim_cols :]
    extended = jnp.concatenate([moments, below_top, above_bottom], axis=1)
    block_span = extended.shape[1]
    window = lax.all_gather(extended, "sub", axis=1, tiled=True)
    target_lists = lax.all_to_all(partners, "sub", split_axis=0, concat_axis=1, tiled=True)
    usable = target_lists >= 0
    slab_cells = cell_count * sub_count
    source_slab = target_lists // slab_cells
    within = target_lists % slab_cells
    source_sub = within // cell_count
    inner = within % cell_count
    delta = source_slab - my_slab
    column = jnp.where(
        delta == 0,
        inner,
        jnp.where(
            delta < 0, inner - (cell_count - rim_cols) + cell_count, inner + cell_count + rim_cols
        ),
    )
    offset_ids = jnp.where(usable, source_sub * block_span + column, 0)
    columns = jnp.take(window, offset_ids, axis=1)
    columns = jnp.where(usable[None, :, :], columns, jnp.zeros((), jnp.bfloat16))
    partial_terms = jnp.einsum("bij,jbc->ic", m2l_ops, columns, preferred_element_type=jnp.float32)
    far_field = lax.psum_scatter(partial_terms, "sub", scatter_dimension=1, tiled=True)
    locals_all = (incoming.astype(jnp.float32) + far_field).astype(jnp.bfloat16)
    child_out = jnp.einsum("oij,jp->ipo", l2l_ops, locals_all, preferred_element_type=jnp.float32)
    return child_out.reshape(order_cube, cell_count * 8)


def solution(mesh):
    in_specs = (
        P(None, ("slab", "sub")),
        P(None, ("slab", "sub")),
        P(),
        P("sub", None, None),
        P(),
        P(None, ("slab", "sub")),
    )
    out_specs = P(None, ("slab", "sub"))
    return jax.shard_map(local, mesh=mesh, in_specs=in_specs, out_specs=out_specs, check_vma=False)
```

profile of v0, /device:TPU:0, one launch (start us, length us, event | category | flops | bytes accessed | tf_op | source)
XLA Modules:
  0.0 168.5 jit_solution(7079776597476378982)
XLA Ops:
  6.5 0.0 copy-start
  6.5 1.3 copy.16
  7.8 1.6 fusion.11
  9.4 0.1 fusion.39
  9.5 2.4 %collective-permute-start = (bf16[216,32]{1,0:T(8,128)(2,1)S(1)}, bf16[216,32]{1,0:T(8,128)(2,1)S(1)}, u32[]{:S(2)}, u32[]{:S(2)}) collective-permute-start(bf16[216,32]{1,0:T(8,128)(2,1)S(1)} %get-tuple-element.7), channel_id=1, source_target_pairs={{0,4},{4,8},{8,12},{12,16},{16,20},{20,24},{24,28},{1,5},{5,9},{9,... | collective-permute-start | bytes 41480 | tf_op jit(solution)/shard_map/ppermute | solution.py:12
  11.9 1.3 collective-permute-start.1
  13.2 4.5 %all-to-all-start = ((s32[4,40,128]{2,1,0:T(8,128)}), s32[4,40,128]{2,1,0:T(8,128)S(1)}, u32[]{:S(2)}, u32[]{:S(2)}) async-start(s32[4,40,128]{2,1,0:T(8,128)} %bitcast.61), calls=%async_computation | async-start | bytes 163840 | tf_op jit(solution)/shard_map/all_to_all | solution.py:37
  17.8 0.0 reduce-scatter.2.cloned.1.call-start
  17.8 0.0 collective-permute-done
  17.8 0.0 collective-permute-done.1
  17.8 0.1 pad_maximum_fusion
  17.9 0.1 copy.18
  18.0 10.8 %all_gather.3 = bf16[216,768]{0,1:T(8,128)(2,1)S(1)} all-gather(bf16[216,192]{0,1:T(8,128)(2,1)S(1)} %copy.18), channel_id=1, replica_groups=mesh['slab'=8,'sub'=4] {'sub'}, dimensions={1}, use_global_device_ids=true | all-gather | bytes 414720 | tf_op jit(solution)/shard_map/all_gather | solution.py:36
  28.8 0.0 all-to-all-done
  28.9 0.2 fusion.21
  29.1 81.2 %gather_fusion = bf16[20480,216]{1,0:T(8,128)(2,1)} fusion(bf16[216,768]{0,1:T(8,128)(2,1)S(1)} %all_gather.3, s32[20480]{0:T(1024)S(1)} %broadcast_clamp_fusion), kind=kCustom, calls=%fused_computation | custom fusion | bytes 17776640 | tf_op jit(solution)/shard_map/jit(_take)/gather | solution.py:53
  110.4 13.1 %copy.20 = bf16[40,512,216]{1,2,0:T(8,128)(2,1)} copy(bf16[40,512,216]{2,1,0:T(8,128)(2,1)} %bitcast.56) | data formatting | bytes 17694720 | tf_op jit(solution)/shard_map/jit(_take)/gather | solution.py:53
  123.5 0.2 compare_and_fusion
  123.7 0.0 copy-start.1
  123.7 8.0 %fusion.8 = f32[216,512]{1,0:T(8,128)} fusion(bf16[40,216,216]{2,1,0:T(8,128)(2,1)} %param.9, bf16[40,512,216]{1,2,0:T(8,128)(2,1)} %copy.20, pred[40,512]{1,0:T(8,128)(4,1)S(1)} %get-tuple-element.6, pred[40,512]{1,0:T(8,128)(4,1)S(1)} %get-tuple-element.5), kind=kOutput, calls=%fused_computation.10 | convolution fusion | flops 1919877120 | bytes 13063168 | tf_op jit(solution)/shard_map/bij,jbc->ic/dot_general | solution.py:55
  131.8 0.0 reduce-scatter.2.cloned.1.call-update
  131.8 26.8 %reduce-scatter.2.cloned.1.call-done = f32[216,128]{1,0:T(8,128)} async-done(((f32[216,512]{1,0:T(8,128)}), f32[216,128]{1,0:T(8,128)}) %reduce-scatter.2.cloned.1.call-update) | async-done | bytes 110608 | tf_op jit(solution)/shard_map/reduce_scatter | solution.py:56
  158.6 0.0 copy-done
  158.6 0.0 copy-done.1
  158.6 1.3 convolution_bitcast_fusion
  159.9 0.5 copy.21
  160.4 1.2 copy.22
  (4 shorter events, 0.1 us)
Async XLA Ops:
  6.5 152.1 %copy-start = (bf16[8,216,216]{2,1,0:T(8,128)(2,1)S(1)}, bf16[8,216,216]{2,1,0:T(8,128)(2,1)}, u32[]{:S(2)}) copy-start(bf16[8,216,216]{2,1,0:T(8,128)(2,1)} %param.10) | copy-start | bytes 2239492
  9.5 8.3 %collective-permute-start = (bf16[216,32]{1,0:T(8,128)(2,1)S(1)}, bf16[216,32]{1,0:T(8,128)(2,1)S(1)}, u32[]{:S(2)}, u32[]{:S(2)}) collective-permute-start(bf16[216,32]{1,0:T(8,128)(2,1)S(1)} %get-tuple-element.7), channel_id=1, source_target_pairs={{0,4},{4,8},{8,12},{12,16},{16,20},{20,24},{24,28},{1,5},{5,9},{9,... | collective-permute-start | bytes 41480 | tf_op jit(solution)/shard_map/ppermute | solution.py:12
  11.9 5.9 %collective-permute-start.1 = (bf16[216,32]{1,0:T(8,128)(2,1)S(1)}, bf16[216,32]{1,0:T(8,128)(2,1)S(1)}, u32[]{:S(2)}, u32[]{:S(2)}) collective-permute-start(bf16[216,32]{1,0:T(8,128)(2,1)S(1)} %get-tuple-element.8), channel_id=1, source_target_pairs={{4,0},{8,4},{12,8},{16,12},{20,16},{24,20},{28,24},{5,1},{9,5},{13... | collective-permute-start | bytes 41480 | tf_op jit(solution)/shard_map/ppermute | solution.py:15
  13.2 15.6 %all-to-all-start = ((s32[4,40,128]{2,1,0:T(8,128)}), s32[4,40,128]{2,1,0:T(8,128)S(1)}, u32[]{:S(2)}, u32[]{:S(2)}) async-start(s32[4,40,128]{2,1,0:T(8,128)} %bitcast.61), calls=%async_computation | async-start | bytes 163840 | tf_op jit(solution)/shard_map/all_to_all | solution.py:37
  17.8 140.9 %reduce-scatter.2.cloned.1.call-start = ((), (), s32[]{:S(2)}) async-start(), calls=%async_computation.2 | async-start | bytes 552960 | tf_op jit(solution)/shard_map/reduce_scatter | solution.py:56
  123.7 34.9 %copy-start.1 = (bf16[216,128]{1,0:T(8,128)(2,1)S(1)}, bf16[216,128]{1,0:T(8,128)(2,1)}, u32[]{:S(2)}) copy-start(bf16[216,128]{1,0:T(8,128)(2,1)} %param.7) | copy-start | bytes 165892
Sparse Core Ops, SparseCore 0:
  131.9 26.6 reduce-scatter.1
where the time goes:
time: 169 us; the launch traced here: 168 us
  local copies, waits for them, and re-layouts  97.6 us (58%)
  waiting for transfers between devices  26.8 us (16%)
  between operations  13.5 us (8%)
  matrix products  10.9 us (6%)
  blocking collectives  10.8 us (6%)
  starting transfers between devices  8.24 us (5%)
    gather x2, local copies, waits for them, and re-layouts, local(): columns = jnp.take(window, offset_ids, axis=1)  94.4 us
    reduce_scatter x1, waiting for transfers between devices, local(): lax.psum_scatter(partial_terms, 'sub', scatter_dimension=1, tiled=True)  26.8 us
    all_gather x1, blocking collectives, local(): window = lax.all_gather(extended, 'sub', axis=1, tiled=True)  10.8 us
    dot_general x1, matrix products, local(): jnp.einsum('bij,jbc->ic', m2l_ops, columns, preferred_element_type=jnp.fl...  8.05 us
    all_to_all x1, starting transfers between devices, local(): lax.all_to_all(partners, 'sub', split_axis=0, concat_axis=1, tiled=True)  4.55 us
  transfers between devices with their start and end apart: 4, of which 1 were waited for; matrix products, arithmetic and copies ran while one was open for 0% of the time, Pallas kernels for 0%

commit v1 on v0

--- a/solution.py
+++ b/solution.py
@@ -33,7 +33,12 @@
     above_bottom = padded[:, padded.shape[1] - rim_cols :]
     extended = jnp.concatenate([moments, below_top, above_bottom], axis=1)
     block_span = extended.shape[1]
-    window = lax.all_gather(extended, "sub", axis=1, tiled=True)
+    ring = [extended]
+    for hop in range(3):
+        ring.append(lax.ppermute(ring[-1], "sub", [(dev, (dev + 1) % 4) for dev in range(4)]))
+    window = jnp.roll(
+        jnp.concatenate(ring[::-1], axis=1), (lax.axis_index("sub") + 1) * ring[0].shape[1], axis=1
+    )
     target_lists = lax.all_to_all(partners, "sub", split_axis=0, concat_axis=1, tiled=True)
     usable = target_lists >= 0
     slab_cells = cell_count * sub_count

time: 169 us -> 178 us (1.053)
  waiting for transfers between devices: 26.8 us -> 42.6 us
  blocking collectives: 10.8 us -> 0 us
  starting transfers between devices: 8.24 us -> 10.6 us
  local copies, waits for them, and re-layouts: 97.6 us -> 99.4 us
    ppermute x0 -> x3, waiting for transfers between devices: none -> 13.7 us  [local(): lax.ppermute(ring[-1], 'sub', [(dev, (dev + 1) % 4) for dev in range(4)])]
    all_gather x1 -> x0, blocking collectives: 10.8 us -> none  [local(): window = lax.all_gather(extended, 'sub', axis=1, tiled=True)]
    all_to_all x1, waiting for transfers between devices: 0.01 us -> 2.71 us  [local(): lax.all_to_all(partners, 'sub', split_axis=0, concat_axis=1, tiled=True)]
    ppermute x0 -> x3, starting transfers between devices: none -> 2.37 us  [local(): lax.ppermute(ring[-1], 'sub', [(dev, (dev + 1) % 4) for dev in range(4)])]
    concatenate x1, local copies, waits for them, and re-layouts: 0.1 us -> 1.89 us  [local(): jnp.roll(jnp.concatenate(ring[::-1], axis=1), (lax.axis_index('sub') + 1)...]
  transfers between devices with their start and end apart: 4 -> 7, of which waited for: 1 -> 5; matrix products, arithmetic and copies ran while one was open for 0% -> 0% of each run, Pallas kernels for 0% -> 0%
where the time goes in v1:
time: 178 us; the launch traced here: 177 us
  local copies, waits for them, and re-layouts  99.4 us (56%)
  waiting for transfers between devices  42.6 us (24%)
  between operations  13.5 us (8%)
  matrix products  10.9 us (6%)
  starting transfers between devices  10.6 us (6%)
    gather x2, local copies, waits for them, and re-layouts, local(): columns = jnp.take(window, offset_ids, axis=1)  93.9 us
    reduce_scatter x1, waiting for transfers between devices, local(): lax.psum_scatter(partial_terms, 'sub', scatter_dimension=1, tiled=True)  26.1 us
    ppermute x3, waiting for transfers between devices, local(): lax.ppermute(ring[-1], 'sub', [(dev, (dev + 1) % 4) for dev in range(4)])  13.7 us
    dot_general x1, matrix products, local(): jnp.einsum('bij,jbc->ic', m2l_ops, columns, preferred_element_type=jnp.fl...  8.05 us
    all_to_all x1, starting transfers between devices, local(): lax.all_to_all(partners, 'sub', split_axis=0, concat_axis=1, tiled=True)  4.55 us
  transfers between devices with their start and end apart: 7, of which 5 were waited for; matrix products, arithmetic and copies ran while one was open for 0% of the time, Pallas kernels for 0%

profile of v1, /device:TPU:0, one launch (start us, length us, event | category | flops | bytes accessed | tf_op | source)
XLA Modules:
  0.0 177.5 jit_solution(833746078150605111)
XLA Ops:
  6.5 0.0 copy-start
  6.5 1.3 copy.16
  7.8 1.6 fusion.11
  9.4 0.1 fusion.39
  9.5 2.4 %collective-permute-start = (bf16[216,32]{1,0:T(8,128)(2,1)S(1)}, bf16[216,32]{1,0:T(8,128)(2,1)S(1)}, u32[]{:S(2)}, u32[]{:S(2)}) collective-permute-start(bf16[216,32]{1,0:T(8,128)(2,1)S(1)} %get-tuple-element.7), channel_id=1, source_target_pairs={{0,4},{4,8},{8,12},{12,16},{16,20},{20,24},{24,28},{1,5},{5,9},{9,... | collective-permute-start | bytes 41480 | tf_op jit(solution)/shard_map/ppermute | solution.py:12
  11.9 1.3 collective-permute-start.1
  13.2 4.5 %all-to-all-start = ((s32[4,40,128]{2,1,0:T(8,128)}), s32[4,40,128]{2,1,0:T(8,128)S(1)}, u32[]{:S(2)}, u32[]{:S(2)}) async-start(s32[4,40,128]{2,1,0:T(8,128)} %bitcast.61), calls=%async_computation | async-start | bytes 163840 | tf_op jit(solution)/shard_map/all_to_all | solution.py:42
  17.8 0.0 reduce-scatter.2.cloned.1.call-start
  17.8 0.0 collective-permute-done
  17.8 0.0 collective-permute-done.1
  17.8 0.1 pad_maximum_fusion
  17.9 2.1 %collective-permute-start.2 = (bf16[216,192]{1,0:T(8,128)(2,1)S(1)}, bf16[216,192]{1,0:T(8,128)(2,1)S(1)}, u32[]{:S(2)}, u32[]{:S(2)}) collective-permute-start(bf16[216,192]{1,0:T(8,128)(2,1)S(1)} %pad_maximum_fusion), channel_id=1, source_target_pairs={{0,1},{1,2},{2,3},{3,0},{4,5},{5,6},{6,7},{7,4},{8,9},{9,10},{10,1... | collective-permute-start | bytes 248840 | tf_op jit(solution)/shard_map/ppermute | solution.py:38
  19.9 2.7 %all-to-all-done = s32[4,40,128]{2,1,0:T(8,128)S(1)} async-done(((s32[4,40,128]{2,1,0:T(8,128)}), s32[4,40,128]{2,1,0:T(8,128)S(1)}, u32[]{:S(2)}, u32[]{:S(2)}) %all-to-all-start) | async-done | bytes 81952 | tf_op jit(solution)/shard_map/all_to_all | solution.py:42
  22.7 0.2 fusion.21
  22.9 1.5 collective-permute-done.2
  24.5 0.3 collective-permute-start.3
  24.8 6.4 %collective-permute-done.3 = bf16[216,192]{1,0:T(8,128)(2,1)S(1)} collective-permute-done((bf16[216,192]{1,0:T(8,128)(2,1)S(1)}, bf16[216,192]{1,0:T(8,128)(2,1)S(1)}, u32[]{:S(2)}, u32[]{:S(2)}) %collective-permute-start.3) | collective-permute-done | bytes 82976 | tf_op jit(solution)/shard_map/ppermute | solution.py:38
  31.2 0.0 collective-permute-start.4
  31.2 0.2 compare_and_fusion
  31.4 5.8 %collective-permute-done.4 = bf16[216,192]{1,0:T(8,128)(2,1)S(1)} collective-permute-done((bf16[216,192]{1,0:T(8,128)(2,1)S(1)}, bf16[216,192]{1,0:T(8,128)(2,1)S(1)}, u32[]{:S(2)}, u32[]{:S(2)}) %collective-permute-start.4) | collective-permute-done | bytes 82976 | tf_op jit(solution)/shard_map/ppermute | solution.py:38
  37.2 1.9 %concatenate.11 = bf16[216,1536]{1,0:T(8,128)(2,1)S(1)} concatenate(bf16[216,192]{1,0:T(8,128)(2,1)S(1)} %collective-permute-done.4, bf16[216,192]{1,0:T(8,128)(2,1)S(1)} %collective-permute-done.3, bf16[216,192]{1,0:T(8,128)(2,1)S(1)} %collective-permute-done.2, bf16[216,128]{1,0:T(8,128)(2,1)S(1)} %fusion.11, bf16[216,32]{1,0:T(8,128)(2,1)S(1)} %collective-permute-done, ...), dimensions={1} | concatenate | bytes 1327104 | tf_op jit(solution)/shard_map/jit(_roll_dynamic)/concatenate | solution.py:39
  39.1 0.2 constant_dynamic-slice_fusion
  39.3 0.2 copy.19
  39.5 80.8 %gather_fusion = bf16[20480,216]{1,0:T(8,128)(2,1)} fusion(bf16[216,768]{0,1:T(8,128)(2,1)S(1)} %copy.19, s32[20480]{0:T(1024)S(1)} %broadcast_clamp_fusion), kind=kCustom, calls=%fused_computation | custom fusion | bytes 17776640 | tf_op jit(solution)/shard_map/jit(_take)/gather | solution.py:58
  120.2 13.2 %copy.20 = bf16[40,512,216]{1,2,0:T(8,128)(2,1)} copy(bf16[40,512,216]{2,1,0:T(8,128)(2,1)} %bitcast.56) | data formatting | bytes 17694720 | tf_op jit(solution)/shard_map/jit(_take)/gather | solution.py:58
  133.4 8.0 %fusion.8 = f32[216,512]{1,0:T(8,128)} fusion(bf16[40,216,216]{2,1,0:T(8,128)(2,1)} %param.9, bf16[40,512,216]{1,2,0:T(8,128)(2,1)} %copy.20, pred[40,512]{1,0:T(8,128)(4,1)S(1)} %get-tuple-element.6, pred[40,512]{1,0:T(8,128)(4,1)S(1)} %get-tuple-element.5), kind=kOutput, calls=%fused_computation.10 | convolution fusion | flops 1919877120 | bytes 13063168 | tf_op jit(solution)/shard_map/bij,jbc->ic/dot_general | solution.py:60
  141.4 0.0 reduce-scatter.2.cloned.1.call-update
  141.5 26.1 %reduce-scatter.2.cloned.1.call-done = f32[216,128]{1,0:T(8,128)} async-done(((f32[216,512]{1,0:T(8,128)}), f32[216,128]{1,0:T(8,128)}) %reduce-scatter.2.cloned.1.call-update) | async-done | bytes 110608 | tf_op jit(solution)/shard_map/reduce_scatter | solution.py:61
  167.6 0.0 copy-done.1
  167.6 1.3 convolution_bitcast_fusion
  168.9 0.5 copy.21
  169.4 1.2 copy.22
  (6 shorter events, 0.1 us)
Async XLA Ops:
  6.5 161.1 %copy-start = (bf16[8,216,216]{2,1,0:T(8,128)(2,1)S(1)}, bf16[8,216,216]{2,1,0:T(8,128)(2,1)}, u32[]{:S(2)}) copy-start(bf16[8,216,216]{2,1,0:T(8,128)(2,1)} %param.10) | copy-start | bytes 2239492
  9.5 8.3 %collective-permute-start = (bf16[216,32]{1,0:T(8,128)(2,1)S(1)}, bf16[216,32]{1,0:T(8,128)(2,1)S(1)}, u32[]{:S(2)}, u32[]{:S(2)}) collective-permute-start(bf16[216,32]{1,0:T(8,128)(2,1)S(1)} %get-tuple-element.7), channel_id=1, source_target_pairs={{0,4},{4,8},{8,12},{12,16},{16,20},{20,24},{24,28},{1,5},{5,9},{9,... | collective-permute-start | bytes 41480 | tf_op jit(solution)/shard_map/ppermute | solution.py:12
  11.9 5.9 %collective-permute-start.1 = (bf16[216,32]{1,0:T(8,128)(2,1)S(1)}, bf16[216,32]{1,0:T(8,128)(2,1)S(1)}, u32[]{:S(2)}, u32[]{:S(2)}) collective-permute-start(bf16[216,32]{1,0:T(8,128)(2,1)S(1)} %get-tuple-element.8), channel_id=1, source_target_pairs={{4,0},{8,4},{12,8},{16,12},{20,16},{24,20},{28,24},{5,1},{9,5},{13... | collective-permute-start | bytes 41480 | tf_op jit(solution)/shard_map/ppermute | solution.py:15
  13.2 9.4 %all-to-all-start = ((s32[4,40,128]{2,1,0:T(8,128)}), s32[4,40,128]{2,1,0:T(8,128)S(1)}, u32[]{:S(2)}, u32[]{:S(2)}) async-start(s32[4,40,128]{2,1,0:T(8,128)} %bitcast.61), calls=%async_computation | async-start | bytes 163840 | tf_op jit(solution)/shard_map/all_to_all | solution.py:42
  17.8 149.9 %reduce-scatter.2.cloned.1.call-start = ((), (), s32[]{:S(2)}) async-start(), calls=%async_computation.2 | async-start | bytes 552960 | tf_op jit(solution)/shard_map/reduce_scatter | solution.py:61
  17.9 6.6 %collective-permute-start.2 = (bf16[216,192]{1,0:T(8,128)(2,1)S(1)}, bf16[216,192]{1,0:T(8,128)(2,1)S(1)}, u32[]{:S(2)}, u32[]{:S(2)}) collective-permute-start(bf16[216,192]{1,0:T(8,128)(2,1)S(1)} %pad_maximum_fusion), channel_id=1, source_target_pairs={{0,1},{1,2},{2,3},{3,0},{4,5},{5,6},{6,7},{7,4},{8,9},{9,10},{10,1... | collective-permute-start | bytes 248840 | tf_op jit(solution)/shard_map/ppermute | solution.py:38
  24.5 6.7 %collective-permute-start.3 = (bf16[216,192]{1,0:T(8,128)(2,1)S(1)}, bf16[216,192]{1,0:T(8,128)(2,1)S(1)}, u32[]{:S(2)}, u32[]{:S(2)}) collective-permute-start(bf16[216,192]{1,0:T(8,128)(2,1)S(1)} %collective-permute-done.2), channel_id=1, source_target_pairs={{0,1},{1,2},{2,3},{3,0},{4,5},{5,6},{6,7},{7,4},{8,9},{9,10},{10,1... | collective-permute-start | bytes 248840 | tf_op jit(solution)/shard_map/ppermute | solution.py:38
  31.2 6.0 %collective-permute-start.4 = (bf16[216,192]{1,0:T(8,128)(2,1)S(1)}, bf16[216,192]{1,0:T(8,128)(2,1)S(1)}, u32[]{:S(2)}, u32[]{:S(2)}) collective-permute-start(bf16[216,192]{1,0:T(8,128)(2,1)S(1)} %collective-permute-done.3), channel_id=1, source_target_pairs={{0,1},{1,2},{2,3},{3,0},{4,5},{5,6},{6,7},{7,4},{8,9},{9,10},{10,1... | collective-permute-start | bytes 248840 | tf_op jit(solution)/shard_map/ppermute | solution.py:38
  133.4 34.2 %copy-start.1 = (bf16[216,128]{1,0:T(8,128)(2,1)S(1)}, bf16[216,128]{1,0:T(8,128)(2,1)}, u32[]{:S(2)}) copy-start(bf16[216,128]{1,0:T(8,128)(2,1)} %param.7) | copy-start | bytes 165892
Sparse Core Ops, SparseCore 0:
  141.6 25.9 reduce-scatter.1
